TPU v7x, 8 devices: a whole 2x2x1 slice. The times are simulated.
8 devices in a mesh: dp: 1 (over z), tx: 2 (over y), tyz: 4 (over x, core).
Axes of the slice: x: 2, y: 2, z: 1, core: 2. Of those that a mesh axis runs over, the one named last changes fastest.
Arguments:
- residual: bfloat16 [512, 4096], P('dp', ('tx', 'tyz'))
- ln_scale: bfloat16 [4096], P(('tx', 'tyz'))
- w_query: bfloat16 [4096, 4096], P('tx', 'tyz')
- w_key: bfloat16 [4096, 256], P('tx')
- w_value: bfloat16 [4096, 256], P('tx')
- w_gate: bfloat16 [4096, 16384], P('tx', 'tyz')
- w_up: bfloat16 [4096, 16384], P('tx', 'tyz')
- w_out: bfloat16 [4096, 4096], P('tyz', 'tx')
- w_down: bfloat16 [16384, 4096], P('tyz', 'tx')
- k_cache: bfloat16 [512, 1024, 256], P(('dp', 'tx', 'tyz'))
- v_cache: bfloat16 [512, 1024, 256], P(('dp', 'tx', 'tyz'))
- lengths: int32 [512], P(('dp', 'tx', 'tyz'))
Outputs:
- output 1: bfloat16 [512, 4096], P('dp', ('tx', 'tyz'))
- output 2: bfloat16 [512, 1024, 256], P(('dp', 'tx', 'tyz'))
- output 3: bfloat16 [512, 1024, 256], P(('dp', 'tx', 'tyz'))
All inputs are finite; a program needn't handle non-finite values.
Results may differ from a plain program's by a relative error of at most 0.0142845.
Values are sent between devices in bfloat16 or wider.
A program may use at most 1 GiB of HBM per device.

v0:
```python
import functools

import jax
import jax.numpy as jnp
import numpy as np
from jax import lax
from jax.experimental import pallas as pl
from jax.experimental.pallas import tpu as pltpu
from jax.sharding import PartitionSpec as P


LN_EPS = 1e-5
ROPE_BASE = 10000.0
MESH = pl.DeviceIdType.MESH
F32 = jnp.float32
BF16 = jnp.bfloat16
SPANS = ((0, 32), (32, 64), (96, 64), (160, 96), (256, 128), (384, 128))
CHUNKS = len(SPANS)
EARLY = 4
SLOTS = 4
WCOLS = 512
SIZES = (80, 80, 64, 32)
STARTS = (0, 80, 160, 224)
PIECES = (2, 4, 4, 4)
HBM = pl.BlockSpec(memory_space=pl.ANY)
ATTN_ROWS = 8


def front_kernel(res_in, ln_in, wq_ref, wk_ref, wv_ref, wg_ref, wu_ref,
                 got_ref, gu1_ref, gu2_ref, gu3_ref, mine0_ref, mine1_ref, mine2_ref, mine3_ref, q_ref, k_ref, v_ref,
                 res_ref, ln_ref, kv_new, raw, hn, wq, wkv, slots, stage, first, stat, stats, lnb, lns, colstat, q_send, q_got, q_own, kv_send, kv_got,
                 stat_send, stat_recv, ln_send, ln_recv, pair_send, pair_recv, x_send, x_recv, relay_send, relay_recv,
                 q_ssem, q_rsem, kv_ssem, kv_rsem, wq_sem, slot_sem, out_sem, first_ssem, first_rsem, a2a_ssem, a2a_rsem, in_sem, new_sem):
    tx = lax.axis_index('tx')
    ty = lax.axis_index('tyz')
    rows, width = res_ref.shape
    half = rows // 2
    model_dim = 8 * width
    pair = ty + 1 - 2 * lax.rem(ty, 2)
    across = lax.rem(ty + 2, 4)
    me = tx * 4 + ty
    few = k_ref.shape[0]
    dim = k_ref.shape[1]
    wcols = slots.shape[2]
    ff = wg_ref.shape[1]
    per = ff // wcols

    def dot(a, b):
        return jnp.dot(a, b, preferred_element_type=F32)

    inputs = [pltpu.make_async_copy(res_in, res_ref, in_sem.at[0]), pltpu.make_async_copy(ln_in, ln_ref, in_sem.at[1])]
    for copy in inputs:
        copy.start()
    weights = [pltpu.make_async_copy(wq_ref, wq, wq_sem.at[0]),
               pltpu.make_async_copy(wk_ref, wkv.at[:, pl.ds(0, dim)], wq_sem.at[1]),
               pltpu.make_async_copy(wv_ref, wkv.at[:, pl.ds(dim, dim)], wq_sem.at[2])]

    def fetch(ref, idx, slot):
        start = pl.multiple_of(idx * wcols, wcols)
        return pltpu.make_async_copy(ref.at[:, pl.ds(start, wcols)], slots.at[slot], slot_sem.at[slot])

    barrier = pltpu.get_barrier_semaphore()
    for off in range(1, 8):
        peer = lax.rem(me + off, 8)
        pl.semaphore_signal(barrier, inc=1, device_id={'tx': peer // 4, 'tyz': lax.rem(peer, 4)}, device_id_type=MESH)
    inputs[0].wait()
    for copy in weights:
        copy.start()
    for idx in range(SLOTS - 1):
        fetch(wg_ref, idx, idx).start()
    inputs[1].wait()
    lnb[...] = jnp.broadcast_to(ln_ref[...].astype(F32)[None, :], lnb.shape).astype(BF16)
    res = res_ref[...].astype(F32)
    row_sum = jnp.sum(res, axis=1, keepdims=True)
    row_sq = jnp.sum(jnp.square(res - row_sum / width), axis=1, keepdims=True)
    lane = lax.broadcasted_iota(jnp.int32, (rows, 128), 1)
    both = jnp.where(lax.rem(lane, 8) < 4, row_sum, row_sq).T[:8]
    sub = lax.rem(lax.broadcasted_iota(jnp.int32, (8, 128), 0), 4)
    packed = both[:, :128]
    for idx in range(1, rows // 128):
        packed = jnp.where(sub == idx, both[:, idx * 128:(idx + 1) * 128], packed)
    stat[...] = packed
    pl.semaphore_wait(barrier, 7)

    def cols(who):
        return pl.ds(pl.multiple_of(who * width, width), width)

    def actual(idx):
        start, size = SPANS[idx]
        start = (1 - tx) * half + start if start < half else tx * half + start - half
        return pl.ds(pl.multiple_of(start, 32), size)

    def block(idx):
        return pl.ds(*SPANS[idx])

    copies = []
    crossing = []
    paired = []
    relayed = []
    for idx in range(CHUNKS):
        crossing.append(pltpu.make_async_remote_copy(
            res_ref.at[actual(idx)], raw.at[block(idx), cols(ty)], x_send.at[idx], x_recv.at[idx],
            device_id={'tyz': across}, device_id_type=MESH))
        paired.append(pltpu.make_async_remote_copy(
            res_ref.at[actual(idx)], raw.at[block(idx), cols(ty)], pair_send.at[idx], pair_recv.at[idx],
            device_id={'tyz': pair}, device_id_type=MESH))
        relayed.append(pltpu.make_async_remote_copy(
            raw.at[block(idx), cols(across)], raw.at[block(idx), cols(across)], relay_send.at[idx], relay_recv.at[idx],
            device_id={'tyz': pair}, device_id_type=MESH))
    stats[me] = stat[...]
    for off in range(1, 8):
        peer = lax.rem(me + off, 8)
        copies.append(pltpu.make_async_remote_copy(
            stat, stats.at[me], stat_send.at[off], stat_recv.at[off],
            device_id={'tx': peer // 4, 'tyz': lax.rem(peer, 4)}, device_id_type=MESH))
    for off in range(1, 4):
        copies.append(pltpu.make_async_remote_copy(
            lnb, lns.at[:, cols(ty)], ln_send.at[off], ln_recv.at[off],
            device_id={'tyz': lax.rem(ty + off, 4)}, device_id_type=MESH))
    for copy in copies:
        copy.start()
    for idx in range(CHUNKS):
        crossing[idx].start()
        paired[idx].start()
    for idx in range(CHUNKS):
        raw[block(idx), cols(ty)] = res_ref[actual(idx), :]
    lns[:, cols(ty)] = lnb[...]
    for copy in copies:
        copy.wait_recv()
    total = stats[0][:4]
    for src in range(1, 8):
        total = total + stats[src][:4]
    mean = total / model_dim
    square = jnp.zeros_like(mean)
    for src in range(8):
        square = square + stats[src][4:] + width * jnp.square(stats[src][:4] / width - mean)
    scale = lax.rsqrt(square / model_dim + LN_EPS)
    upper = lax.broadcasted_iota(jnp.int32, (128, 128), 0) < 64
    for idx in range(rows // 128):
        colstat[idx * 128:(idx + 1) * 128, :] = jnp.where(upper, mean[idx:idx + 1], scale[idx:idx + 1]).T

    def norm(idx):
        centre = colstat[actual(idx), :][:, :1]
        factor = colstat[actual(idx), :][:, 64:65]
        for col in range(4):
            part = pl.ds(col * width, width)
            hn[block(idx), part] = ((raw[block(idx), part].astype(F32) - centre) * factor
                                    * lns[:1, part].astype(F32)).astype(BF16)

    q_copies = []
    for idx in range(EARLY):
        crossing[idx].wait_recv()
        relayed[idx].start()
        paired[idx].wait_recv()
        relayed[idx].wait_recv()
        norm(idx)
        if idx == 0:
            weights[0].wait()
        q_send[block(idx), :] = dot(hn[block(idx), :], wq[...]).astype(BF16)
        copy = pltpu.make_async_remote_copy(
            q_send.at[block(idx)], q_got.at[block(idx)], q_ssem.at[idx], q_rsem.at[idx],
            device_id={'tx': 1 - tx}, device_id_type=MESH)
        copy.start()
        q_copies.append(copy)
    weights[1].wait()
    weights[2].wait()
    mine_few = pl.ds(pl.multiple_of(ty * few, few), few)
    kv_send[...] = dot(hn[mine_few, :], wkv[...]).astype(BF16)
    kv_copy = pltpu.make_async_remote_copy(kv_send, kv_got, kv_ssem, kv_rsem, device_id={'tx': 1 - tx}, device_id_type=MESH)
    kv_copy.start()

    for idx in range(EARLY, CHUNKS):
        crossing[idx].wait_recv()
        relayed[idx].start()
    for idx in range(EARLY, CHUNKS):
        paired[idx].wait_recv()
        relayed[idx].wait_recv()
        norm(idx)

    outs = ((gu1_ref, STARTS[1]), (gu2_ref, STARTS[2]), (gu3_ref, STARTS[3]), (mine0_ref, half), (mine1_ref, half + STARTS[1]),
            (mine2_ref, half + STARTS[2]), (mine3_ref, half + STARTS[3]))

    def columns(step):
        return pl.ds(pl.multiple_of(step * wcols, wcols), wcols)

    def put(step, slot):
        return [pltpu.make_async_copy(stage.at[slot, pl.ds(start, out.shape[0])], out.at[:, columns(step)], out_sem.at[slot, idx])
                for idx, (out, start) in enumerate(outs)]

    def send_first(step):
        return pltpu.make_async_remote_copy(
            first.at[:, columns(step)], got_ref.at[:, columns(step)], first_ssem.at[step], first_rsem.at[step],
            device_id={'tx': 1 - tx}, device_id_type=MESH)

    def body(step, carry, gate):
        slot = lax.rem(step, SLOTS)
        side = lax.rem(step, 2)
        ahead = step + SLOTS - 1
        into = lax.rem(ahead, SLOTS)
        if gate:
            @pl.when(ahead < per)
            def _():
                fetch(wg_ref, ahead, into).start()

            @pl.when(ahead >= per)
            def _():
                fetch(wu_ref, ahead - per, into).start()

            fetch(wg_ref, 0, slot).wait()
        else:
            @pl.when(ahead < 2 * per)
            def _():
                fetch(wu_ref, ahead - per, into).start()

            fetch(wu_ref, 0, slot).wait()

        @pl.when(step >= 2)
        def _():
            for copy in put(step - 2, side):
                copy.wait()

        stage[side] = dot(hn[...], slots[slot]).astype(BF16)
        for copy in put(step, side):
            copy.start()
        first[:, columns(step)] = stage[side, :SIZES[0], :]
        send_first(step).start()
        return carry

    lax.fori_loop(0, per, functools.partial(body, gate=True), 0)
    q_own[...] = dot(hn[half:, :], wq[...]).astype(BF16)
    own_few = pl.ds(pl.multiple_of(half + ty * few, few), few)
    kv_own = dot(hn[own_few, :], wkv[...])
    kv_copy.wait()
    kv = (kv_own + kv_got[...].astype(F32)).astype(BF16)
    kv_new[0] = kv[:, :dim]
    kv_new[1] = kv[:, dim:]
    for copy in q_copies:
        copy.wait()
    q_own[...] = (q_own[...].astype(F32) + q_got[...].astype(F32)).astype(BF16)
    news = [pltpu.make_async_copy(kv_new.at[0], k_ref, new_sem.at[0]), pltpu.make_async_copy(kv_new.at[1], v_ref, new_sem.at[1]),
            pltpu.make_async_copy(q_own.at[mine_few], q_ref.at[ty], new_sem.at[2])]
    spread = []
    for off in (2, 1, 3):
        peer = lax.rem(ty + off, 4)
        spread.append(pltpu.make_async_remote_copy(
            q_own.at[pl.ds(pl.multiple_of(peer * few, few), few)], q_ref.at[ty], a2a_ssem.at[off], a2a_rsem.at[off],
            device_id={'tyz': peer}, device_id_type=MESH))
    for copy in spread + news:
        copy.start()
    lax.fori_loop(per, 2 * per, functools.partial(body, gate=False), 0)
    for copy in spread + news:
        copy.wait()
    for copy in copies + crossing + paired + relayed:
        copy.wait_send()
    for step in (2 * per - 2, 2 * per - 1):
        for copy in put(step, step % 2):
            copy.wait()
    for step in range(2 * per):
        send_first(step).wait()


def front(residual, ln_scale, w_query, w_key, w_value, w_gate, w_up, few):
    rows, width = residual.shape
    half = rows // 2
    depth, q_cols = w_query.shape
    dim = w_key.shape[1]
    ff = w_gate.shape[1]
    dma = pltpu.SemaphoreType.DMA
    shape = jax.ShapeDtypeStruct
    blocks = tuple(shape((size, 2 * ff), BF16) for size in SIZES)
    return pl.pallas_call(
        front_kernel,
        out_shape=blocks + blocks + (shape((4, few, q_cols), BF16), shape((few, dim), BF16), shape((few, dim), BF16)),
        in_specs=[HBM] * 7,
        out_specs=(HBM,) * 11,
        scratch_shapes=[
            pltpu.VMEM((rows, width), BF16), pltpu.VMEM((width,), BF16), pltpu.VMEM((2, few, dim), BF16),
            pltpu.VMEM((rows, depth), BF16), pltpu.VMEM((rows, depth), BF16),
            pltpu.VMEM((depth, q_cols), BF16), pltpu.VMEM((depth, 2 * dim), BF16),
            pltpu.VMEM((SLOTS, depth, WCOLS), BF16), pltpu.VMEM((2, rows, WCOLS), BF16), pltpu.VMEM((SIZES[0], 2 * ff), BF16),
            pltpu.VMEM((8, 128), F32), pltpu.VMEM((8, 8, 128), F32),
            pltpu.VMEM((16, width), BF16), pltpu.VMEM((16, depth), BF16), pltpu.VMEM((rows, 128), F32),
            pltpu.VMEM((half, q_cols), BF16), pltpu.VMEM((half, q_cols), BF16), pltpu.VMEM((half, q_cols), BF16),
            pltpu.VMEM((few, 2 * dim), BF16), pltpu.VMEM((few, 2 * dim), BF16),
            dma((8,)), dma((8,)), dma((4,)), dma((4,)), dma((CHUNKS,)), dma((CHUNKS,)), dma((CHUNKS,)), dma((CHUNKS,)),
            dma((CHUNKS,)), dma((CHUNKS,)), dma((CHUNKS,)), dma((CHUNKS,)), dma, dma, dma((3,)), dma((SLOTS,)), dma((2, 7)),
            dma((2 * ff // WCOLS,)), dma((2 * ff // WCOLS,)), dma((4,)), dma((4,)), dma((2,)), dma((3,))],
        compiler_params=pltpu.CompilerParams(collective_id=0, has_side_effects=True),
        cost_estimate=pl.CostEstimate(flops=2 ** 34, bytes_accessed=2 ** 26, transcendentals=0),
        name='front',
    )(residual, ln_scale, w_query, w_key, w_value, w_gate, w_up)


def attend_kernel(len_ref, freq_ref, q_ref, knew_ref, vnew_ref, kc_ref, vc_ref, o_ref, kout_ref, vout_ref, q_low, q_high, k_rot, v_new, o_low, o_high):
    step = pl.program_id(0)
    groups, rows, span = q_ref.shape
    seq, dim = kc_ref.shape[1:]
    heads = groups * span // dim
    half = dim // 2
    sub = lax.broadcasted_iota(jnp.int32, (rows, 1), 0)
    positions = jnp.zeros((rows, 1), jnp.int32)
    for row in range(rows):
        positions = jnp.where(sub == row, len_ref[step * rows + row], positions)
    angles = positions.astype(F32) * freq_ref[...]
    cos_part = jnp.cos(angles)
    sin_part = jnp.sin(angles)

    def rotate(first, second):
        first = first.astype(F32)
        second = second.astype(F32)
        return first * cos_part - second * sin_part, second * cos_part + first * sin_part

    k_rot[:, :half], k_rot[:, half:] = rotate(knew_ref[:, :half], knew_ref[:, half:])
    v_new[...] = vnew_ref[...].astype(F32)
    for head in range(heads):
        group, start = divmod(head * dim, span)
        place = pl.ds(head * rows, rows)
        q_low[place, :], q_high[place, :] = rotate(q_ref[group, :, start:start + half], q_ref[group, :, start + half:start + dim])
    for row in range(rows):
        pos = len_ref[step * rows + row]
        start = pl.multiple_of((pos // 16) * 16, 16)
        hit = lax.broadcasted_iota(jnp.int32, (16, 1), 0) == pos - start
        for cache, new, out in ((kc_ref, k_rot, kout_ref), (vc_ref, v_new, vout_ref)):
            out[row] = cache[row]
            window = cache[row, pl.ds(start, 16), :].astype(F32)
            out[row, pl.ds(start, 16), :] = jnp.where(hit, new[row:row + 1, :], window).astype(BF16)
    for row in range(rows):
        pos = len_ref[step * rows + row]
        place = pl.ds(row, heads, stride=rows)
        query = jnp.concatenate([q_low[place, :], q_high[place, :]], axis=1).astype(BF16)
        scores = lax.dot_general(query, kout_ref[row], (((1,), (1,)), ((), ())), preferred_element_type=F32) * dim ** -0.5
        where = lax.broadcasted_iota(jnp.int32, (1, seq), 1) <= pos
        scores = jnp.where(where, scores, -1e30)
        top = jnp.max(scores, axis=1, keepdims=True)
        weight = jnp.exp(scores - top)
        probs = (weight / jnp.sum(weight, axis=1, keepdims=True)).astype(BF16)
        total = jnp.dot(probs, vout_ref[row], preferred_element_type=F32)
        o_low[place, :] = total[:, :half]
        o_high[place, :] = total[:, half:]
    for head in range(heads):
        o_ref[:, head * dim:head * dim + half] = o_low[head * rows:(head + 1) * rows, :].astype(BF16)
        o_ref[:, head * dim + half:(head + 1) * dim] = o_high[head * rows:(head + 1) * rows, :].astype(BF16)


def attend(lengths, query, key_new, value_new, k_cache, v_cache):
    groups, rows, span = query.shape
    seq, dim = k_cache.shape[1:]
    width = groups * span
    freq = jnp.asarray(np.power(ROPE_BASE, -2.0 * np.arange(dim // 2) / dim)[None, :].astype(np.float32))
    new = pl.BlockSpec((ATTN_ROWS, dim), lambda i, lens: (i, 0))
    big = pl.BlockSpec((ATTN_ROWS, seq, dim), lambda i, lens: (i, 0, 0))
    return pl.pallas_call(
        attend_kernel,
        grid_spec=pltpu.PrefetchScalarGridSpec(
            num_scalar_prefetch=1, grid=(rows // ATTN_ROWS,),
            in_specs=[pl.BlockSpec((1, dim // 2), lambda i, lens: (0, 0)),
                      pl.BlockSpec((groups, ATTN_ROWS, span), lambda i, lens: (0, i, 0)), new, new, big, big],
            out_specs=[pl.BlockSpec((ATTN_ROWS, width), lambda i, lens: (i, 0)), big, big],
            scratch_shapes=[pltpu.VMEM((ATTN_ROWS * width // dim, dim // 2), F32)] * 2 + [pltpu.VMEM((ATTN_ROWS, dim), F32)] * 2
            + [pltpu.VMEM((ATTN_ROWS * width // dim, dim // 2), F32)] * 2),
        out_shape=(jax.ShapeDtypeStruct((rows, width), BF16),
                   jax.ShapeDtypeStruct(k_cache.shape, BF16),
                   jax.ShapeDtypeStruct(v_cache.shape, BF16)),
        compiler_params=pltpu.CompilerParams(vmem_limit_bytes=67043328),
        cost_estimate=pl.CostEstimate(flops=2 ** 33, bytes_accessed=2 ** 27, transcendentals=2 ** 20),
        name='attend',
    )(lengths, freq, query, key_new, value_new, k_cache, v_cache)


def tail_kernel(act0_ref, act1_ref, act2_ref, got_ref, mine_ref, att_in, wo_ref, wd_ref, res_in, out_ref,
                att_ref, res_ref, wo, wd, gu_got, gu_mine, act, act_got, o_mine, o_got, sums, out_buf,
                send_own, recv_own, keep_own, send0, recv0, keep0, send1, recv1, keep1, send2, recv2, keep2, send3, recv3, keep3,
                w_sem, gu_sem, o_ssem, o_rsem, a2a_ssem, a2a_rsem, act_ssem, act_rsem, own_ssem, own_rsem, row_ssem, row_rsem, out_sem):
    tx = lax.axis_index('tx')
    ty = lax.axis_index('tyz')
    few = att_ref.shape[0]
    half = 4 * few
    width = out_ref.shape[1]
    ff = act.shape[1]
    o_cols = o_mine.shape[1]
    acts = (act0_ref, act1_ref, act2_ref)

    def dot(a, b):
        return jnp.dot(a, b, preferred_element_type=F32)

    def peer_of(rel):
        return 2 * lax.rem(ty // 2 + rel // 2, 2) + lax.rem(lax.rem(ty, 2) + lax.rem(rel, 2), 2)

    weights = [pltpu.make_async_copy(wo_ref, wo, w_sem.at[0]), pltpu.make_async_copy(wd_ref, wd, w_sem.at[1]),
               pltpu.make_async_copy(res_in, res_ref, w_sem.at[2])]
    att_copy = pltpu.make_async_copy(att_in, att_ref, w_sem.at[3])
    loads = [pltpu.make_async_copy(mine_ref, gu_mine, gu_sem.at[3]), pltpu.make_async_copy(got_ref, gu_got, gu_sem.at[4])]
    held = [pltpu.make_async_copy(ref, act.at[pl.ds(STARTS[idx], SIZES[idx])], gu_sem.at[idx]) for idx, ref in enumerate(acts)]
    barrier = pltpu.get_barrier_semaphore()
    pl.semaphore_signal(barrier, inc=1, device_id={'tx': 1 - tx}, device_id_type=MESH)
    for rel in (1, 2, 3):
        pl.semaphore_signal(barrier, inc=1, device_id={'tyz': peer_of(rel)}, device_id_type=MESH)

    def silu(col, carry):
        part = pl.ds(pl.multiple_of(col * 512, 512), 512)
        other = pl.ds(pl.multiple_of(ff + col * 512, 512), 512)
        gate = (gu_mine[:, part].astype(F32) + gu_got[:, part].astype(F32)).astype(BF16).astype(F32)
        up = (gu_mine[:, other].astype(F32) + gu_got[:, other].astype(F32)).astype(BF16).astype(F32)
        act[STARTS[3]:, part] = (gate / (1.0 + jnp.exp(-gate)) * up).astype(BF16)
        return carry

    def act_copy(idx, where):
        piece = ff // PIECES[idx]
        sem = sum(PIECES[:idx]) + where
        span = pl.ds(pl.multiple_of(where * piece, piece), piece)
        rows = pl.ds(STARTS[idx], SIZES[idx])
        src = acts[idx].at[:, span] if idx < 3 else act.at[rows, span]
        return pltpu.make_async_remote_copy(src, act_got.at[rows, span], act_ssem.at[sem], act_rsem.at[sem],
                                            device_id={'tx': 1 - tx}, device_id_type=MESH)

    def columns(who, count):
        return pl.ds(pl.multiple_of(who * count, count), count)

    for copy in [att_copy] + loads:
        copy.start()
    pl.semaphore_wait(barrier, 4)
    for where in range(PIECES[0]):
        act_copy(0, where).start()
    att_copy.wait()
    o_spread = []
    for rel in (2, 3, 1):
        o_spread.append(pltpu.make_async_remote_copy(
            att_ref.at[:, columns(peer_of(rel), o_cols)], o_mine.at[columns(ty, few)], a2a_ssem.at[rel], a2a_rsem.at[rel],
            device_id={'tyz': peer_of(rel)}, device_id_type=MESH))
    for copy in o_spread:
        copy.start()
    for copy in held + weights:
        copy.start()
    o_mine[columns(ty, few), :] = att_ref[:, columns(ty, o_cols)]
    for copy in loads:
        copy.wait()
    lax.fori_loop(0, ff // 512, silu, 0)
    for copy in o_spread:
        copy.wait()
    o_copy = pltpu.make_async_remote_copy(o_mine, o_got, o_ssem, o_rsem, device_id={'tx': 1 - tx}, device_id_type=MESH)
    o_copy.start()
    for idx in (1, 2, 3):
        for where in range(PIECES[idx]):
            act_copy(idx, where).start()
    for copy in held + weights:
        copy.wait()

    def ship(rel, src, dst, ssem, rsem):
        return pltpu.make_async_remote_copy(src.at[rel], dst.at[rel], ssem.at[rel], rsem.at[rel],
                                            device_id={'tyz': peer_of(rel)}, device_id_type=MESH)

    def spread(value, src, dst, kept, ssem, rsem):
        def body(step, carry):
            rel = lax.rem(step + 2, 4)
            total = value(columns(peer_of(rel), width))

            @pl.when(rel == 0)
            def _():
                kept[...] = total

            @pl.when(rel != 0)
            def _():
                src[rel] = total.astype(BF16)
                ship(rel, src, dst, ssem, rsem).start()

            return carry

        lax.fori_loop(0, 4, body, 0)

    outs = []

    def finish(start, src, dst, kept, ssem, rsem):
        total = kept[...]
        for rel in (1, 2, 3):
            ship(rel, src, dst, ssem, rsem).wait()
        for rel in (1, 2, 3):
            total = total + dst[rel].astype(F32)
        rows = pl.ds(pl.multiple_of(start, 16), total.shape[0])
        out_ref[rows, :] = (res_ref[rows, :].astype(F32) + total).astype(out_ref.dtype)

    own = (send_own, recv_own, keep_own, own_ssem, own_rsem)
    blocks = [(src, dst, kept, row_ssem.at[idx], row_rsem.at[idx]) for idx, (src, dst, kept) in enumerate(
        ((send0, recv0, keep0), (send1, recv1, keep1), (send2, recv2, keep2), (send3, recv3, keep3)))]
    base = (1 - tx) * half
    spread(lambda cols: dot(o_mine[...], wo[:, cols]) + dot(act[...], wd[:, cols]), *own)
    for idx in range(4):
        piece = ff // PIECES[idx]
        last = PIECES[idx] - 1
        size = SIZES[idx]
        rows = slice(STARTS[idx], STARTS[idx] + size)
        if idx == 0:
            sums[:size, :] = jnp.zeros((size, sums.shape[1]), F32)
        else:
            sums[:size, :] = dot(o_got[rows, :], wo[...])

        def body(where, carry, idx=idx, piece=piece, rows=rows, size=size):
            act_copy(idx, where).wait_recv()
            span = pl.ds(pl.multiple_of(where * piece, piece), piece)
            sums[:size, :] += dot(act_got[rows, span], wd[span, :])
            return carry

        lax.fori_loop(0, last, body, 0)
        act_copy(idx, last).wait_recv()
        if idx == 0:
            finish(tx * half, *own)
            o_copy.wait_recv()
            sums[:size, :] += dot(o_got[rows, :], wo[...])
        spread(lambda cols: sums[:size, cols] + dot(act_got[rows, last * piece:], wd[last * piece:, cols]), *blocks[idx])
        if idx > 0:
            finish(base + STARTS[idx - 1], *blocks[idx - 1])
    finish(base + STARTS[3], *blocks[3])
    o_copy.wait_send()
    for idx in range(4):
        for where in range(PIECES[idx]):
            act_copy(idx, where).wait_send()
    for copy in outs:
        copy.wait()


def activation(mine, got):
    ff = mine.shape[1] // 2
    gate = (mine[:, :ff].astype(F32) + got[:, :ff].astype(F32)).astype(BF16).astype(F32)
    up = (mine[:, ff:].astype(F32) + got[:, ff:].astype(F32)).astype(BF16).astype(F32)
    return (jax.nn.silu(gate) * up).astype(BF16)


def tail(acts, got, mine, attended, w_out, w_down, residual):
    few = attended.shape[0]
    half = 4 * few
    o_cols = w_out.shape[0]
    ff, out_cols = w_down.shape
    _, width = residual.shape
    dma = pltpu.SemaphoreType.DMA
    count = sum(PIECES)
    exchange = []
    for size in (half,) + SIZES:
        exchange += [pltpu.VMEM((4, size, width), BF16), pltpu.VMEM((4, size, width), BF16), pltpu.VMEM((size, width), F32)]
    return pl.pallas_call(
        tail_kernel,
        out_shape=jax.ShapeDtypeStruct(residual.shape, residual.dtype),
        in_specs=[HBM] * 9,
        out_specs=pl.BlockSpec(memory_space=pltpu.VMEM),
        scratch_shapes=[pltpu.VMEM(attended.shape, BF16), pltpu.VMEM(residual.shape, residual.dtype), pltpu.VMEM(w_out.shape, BF16), pltpu.VMEM(w_down.shape, BF16),
                        pltpu.VMEM((SIZES[3], 2 * ff), BF16), pltpu.VMEM((SIZES[3], 2 * ff), BF16),
                        pltpu.VMEM((half, ff), BF16), pltpu.VMEM((half, ff), BF16),
                        pltpu.VMEM((half, o_cols), BF16), pltpu.VMEM((half, o_cols), BF16), pltpu.VMEM((SIZES[0], out_cols), F32),
                        pltpu.VMEM(residual.shape, residual.dtype)] + exchange
        + [dma((4,)), dma((5,)), dma, dma, dma((4,)), dma((4,)), dma((count,)), dma((count,)),
           dma((4,)), dma((4,)), dma((4, 4)), dma((4, 4)), dma((5,))],
        compiler_params=pltpu.CompilerParams(collective_id=1, has_side_effects=True, vmem_limit_bytes=50 * 2 ** 20),
        cost_estimate=pl.CostEstimate(flops=2 ** 34, bytes_accessed=2 ** 25, transcendentals=0),
        name='tail',
    )(*acts, got, mine, attended, w_out, w_down, residual)


def solution(mesh):


    row_axes = ('dp', 'tx', 'tyz')
    swap = [(0, 1), (1, 0)]

    def decode_layer(residual, ln_scale, w_query, w_key, w_value, w_gate, w_up, w_out, w_down, k_cache, v_cache, lengths):
        rows_local = k_cache.shape[0]

        def pass_on(x):
            return lax.ppermute(x, 'tx', swap)

        got, *rest = front(residual, ln_scale, w_query, w_key, w_value, w_gate, w_up, rows_local)
        gots = [got]
        for idx in range(3):
            gots.append(pass_on(rest[idx]))
        mines = rest[3:7]
        query_mine, key_new, value_new = rest[7:]
        attended, k_updated, v_updated = attend(lengths, query_mine, key_new, value_new, k_cache, v_cache)
        acts = [activation(mines[idx], gots[idx]) for idx in range(3)]
        new_resid = tail(acts, gots[3], mines[3], attended, w_out, w_down, residual)
        return new_resid, k_updated, v_updated

    in_specs = (P('dp', ('tx', 'tyz')), P(('tx', 'tyz')), P('tx', 'tyz'), P('tx', None), P('tx', None), P('tx', 'tyz'), P('tx', 'tyz'), P('tyz', 'tx'), P('tyz', 'tx'), P(row_axes, None, None), P(row_axes, None, None), P(row_axes))
    out_specs = (P('dp', ('tx', 'tyz')), P(row_axes, None, None), P(row_axes, None, None))
    return jax.shard_map(decode_layer, mesh=mesh, in_specs=in_specs, out_specs=out_specs, check_vma=False)
```

profile of v0, /device:TPU:0, one launch (start us, length us, event | category | flops | bytes accessed | tf_op | source)
XLA Modules:
  0.0 186.3 jit_solution(15611711089355595420)
XLA Ops:
  0.6 54.6 %front.1 = (bf16[80,8192]{1,0:T(8,128)(2,1)}, bf16[80,8192]{1,0:T(8,128)(2,1)}, bf16[64,8192]{1,0:T(8,128)(2,1)}, bf16[32,8192]{1,0:T(8,128)(2,1)}, bf16[80,8192...) custom-call(bf16[512,512]{1,0:T(8,128)(2,1)} %res_in.3, ...), custom_call_target="tpu_custom_call" | custom-call | flops 17179869184 | bytes 67108864 | tf_op jit(solution)/shard_map/front/pallas_call | solution.py:271
  55.2 0.7 collective-permute-start.2
  56.0 1.3 collective-permute-start.1
  57.3 0.7 collective-permute-start
  58.0 3.0 %fusion.9.act0_ref = bf16[80,4096]{1,0:T(8,128)(2,1)} fusion(bf16[80,8192]{1,0:T(8,128)(2,1)} %get-tuple-element.18, bf16[80,8192]{1,0:T(8,128)(2,1)} %get-tuple-element.17), kind=kLoop, calls=%fused_computation.19 | loop fusion | flops 5242880 | bytes 3276800 | tf_op jit(solution)/shard_map/convert_element_type | solution.py:524
  61.1 47.4 %attend.1 = (bf16[64,4096]{1,0:T(8,128)(2,1)}, bf16[64,1024,256]{2,1,0:T(8,128)(2,1)}, bf16[64,1024,256]{2,1,0:T(8,128)(2,1)}) custom-call(s32[64]{0:T(128)} %len_ref.1, f32[1,128]{1,0:T(1,128)} %constant.8.clone.freq_ref, bf16[4,64,1024]{2,1,0:T(8,128)(2,1)} %get-tuple-element.25.q_ref, bf16[64,256]{1,0:T(8,128)(2,1)} %get-tuple-element.26.knew_ref, ...), custom_call_target="tpu_custom_call" | custom-call | flops 8589934592 | bytes 134217728 | tf_op jit(solution)/shard_map/attend/pallas_call | solution.py:352
  108.5 0.0 collective-permute-done.1
  108.5 0.0 copy-start.4
  108.5 2.0 %fusion.14.act2_ref = bf16[64,4096]{1,0:T(8,128)(2,1)S(1)} fusion(bf16[64,8192]{1,0:T(8,128)(2,1)} %collective-permute-done.1, bf16[64,8192]{1,0:T(8,128)(2,1)} %get-tuple-element.21), kind=kLoop, calls=%fused_computation.26 | loop fusion | flops 4194304 | bytes 2621440 | tf_op jit(solution)/shard_map/convert_element_type | solution.py:524
  110.5 9.1 %collective-permute-done = bf16[80,8192]{1,0:T(8,128)(2,1)} collective-permute-done((bf16[80,8192]{1,0:T(8,128)(2,1)}, bf16[80,8192]{1,0:T(8,128)(2,1)}, u32[]{:S(2)}, u32[]{:S(2)}) %collective-permute-start) | collective-permute-done | bytes 1310752 | tf_op jit(solution)/shard_map/ppermute | solution.py:566
  119.7 0.0 copy-done.4
  119.7 0.0 copy-start
  119.7 0.0 copy-start.1
  119.7 0.0 copy-start.2
  119.7 0.0 copy-start.3
  119.7 2.8 %fusion.8.act1_ref = bf16[80,4096]{1,0:T(8,128)(2,1)} fusion(bf16[80,8192]{1,0:T(8,128)(2,1)} %collective-permute-done, bf16[80,8192]{1,0:T(8,128)(2,1)S(1)} %copy-done.4), kind=kLoop, calls=%fused_computation.18 | loop fusion | flops 5242880 | bytes 3276800 | tf_op jit(solution)/shard_map/convert_element_type | solution.py:524
  122.5 0.0 collective-permute-done.2.got_ref
  122.5 0.0 copy-done
  122.5 0.0 copy-done.1
  122.5 0.0 copy-done.2
  122.5 0.0 copy-done.3
  122.6 63.0 %tail.1 = bf16[512,512]{1,0:T(8,128)(2,1)S(1)} custom-call(bf16[80,4096]{1,0:T(8,128)(2,1)S(1)} %copy-done, bf16[80,4096]{1,0:T(8,128)(2,1)} %fusion.8.act1_ref, bf16[64,4096]{1,0:T(8,128)(2,1)S(1)} %fusion.14.act2_ref, bf16[32,8192]{1,0:T(8,128)(2,1)} %collective-permute-done.2.got_ref, bf16[32,8192]{1,0:T(8,128)(2,1)S(1)} %copy-done.3, ...), custom_call_target="tpu_custom_call" | custom-call | flops 17179869184 | bytes 33554432 | tf_op jit(solution)/shard_map/tail/pallas_call | solution.py:538
  185.6 0.8 copy.17
Async XLA Ops:
  55.2 67.3 %collective-permute-start.2 = (bf16[32,8192]{1,0:T(8,128)(2,1)}, bf16[32,8192]{1,0:T(8,128)(2,1)}, u32[]{:S(2)}, u32[]{:S(2)}) collective-permute-start(bf16[32,8192]{1,0:T(8,128)(2,1)} %get-tuple-element.23), channel_id=1, source_target_pairs={{0,4},{4,0},{1,5},{5,1},{2,6},{6,2},{3,7},{7,3}} | collective-permute-start | bytes 1572872 | tf_op jit(solution)/shard_map/ppermute | solution.py:566
  56.0 52.5 %collective-permute-start.1 = (bf16[64,8192]{1,0:T(8,128)(2,1)}, bf16[64,8192]{1,0:T(8,128)(2,1)}, u32[]{:S(2)}, u32[]{:S(2)}) collective-permute-start(bf16[64,8192]{1,0:T(8,128)(2,1)} %get-tuple-element.22), channel_id=1, source_target_pairs={{0,4},{4,0},{1,5},{5,1},{2,6},{6,2},{3,7},{7,3}} | collective-permute-start | bytes 3145736 | tf_op jit(solution)/shard_map/ppermute | solution.py:566
  57.3 62.4 %collective-permute-start = (bf16[80,8192]{1,0:T(8,128)(2,1)}, bf16[80,8192]{1,0:T(8,128)(2,1)}, u32[]{:S(2)}, u32[]{:S(2)}) collective-permute-start(bf16[80,8192]{1,0:T(8,128)(2,1)} %get-tuple-element.20), channel_id=1, source_target_pairs={{0,4},{4,0},{1,5},{5,1},{2,6},{6,2},{3,7},{7,3}} | collective-permute-start | bytes 3932168 | tf_op jit(solution)/shard_map/ppermute | solution.py:566
  108.5 11.2 %copy-start.4 = (bf16[80,8192]{1,0:T(8,128)(2,1)S(1)}, bf16[80,8192]{1,0:T(8,128)(2,1)}, u32[]{:S(2)}) copy-start(bf16[80,8192]{1,0:T(8,128)(2,1)} %get-tuple-element.19) | copy-start | bytes 3932164
  119.7 2.9 %copy-start = (bf16[80,4096]{1,0:T(8,128)(2,1)S(1)}, bf16[80,4096]{1,0:T(8,128)(2,1)}, u32[]{:S(2)}) copy-start(bf16[80,4096]{1,0:T(8,128)(2,1)} %fusion.9.act0_ref) | copy-start | bytes 1966084
  119.7 2.9 %copy-start.1 = (bf16[512,512]{1,0:T(8,128)(2,1)S(1)}, bf16[512,512]{1,0:T(8,128)(2,1)}, u32[]{:S(2)}) copy-start(bf16[512,512]{1,0:T(8,128)(2,1)} %res_in.3) | copy-start | bytes 1572868
  119.7 2.9 %copy-start.2 = (bf16[64,4096]{1,0:T(8,128)(2,1)S(1)}, bf16[64,4096]{1,0:T(8,128)(2,1)}, u32[]{:S(2)}) copy-start(bf16[64,4096]{1,0:T(8,128)(2,1)} %get-tuple-element.28.att_in) | copy-start | bytes 1572868
  119.7 2.9 %copy-start.3 = (bf16[32,8192]{1,0:T(8,128)(2,1)S(1)}, bf16[32,8192]{1,0:T(8,128)(2,1)}, u32[]{:S(2)}) copy-start(bf16[32,8192]{1,0:T(8,128)(2,1)} %get-tuple-element.24.mine_ref) | copy-start | bytes 1572868
where the time goes:
time: 187 us; the launch traced here: 186 us
  Pallas kernels  165 us (88%)
  waiting for transfers between devices  9.13 us (5%)
  other arithmetic  7.93 us (4%)
  starting transfers between devices  2.76 us (1%)
    pallas_call x1, Pallas kernels, tail(): pl.pallas_call(tail_kernel, out_shape=jax.ShapeDtypeStruct(residual.shape...  63 us
    pallas_call x1, Pallas kernels, front(): pl.pallas_call(front_kernel, out_shape=blocks + blocks + (shape((4, few,...  54.6 us
    pallas_call x1, Pallas kernels, attend(): pl.pallas_call(attend_kernel, grid_spec=pltpu.PrefetchScalarGridSpec(num_...  47.4 us
    ppermute x3, waiting for transfers between devices, pass_on(): return lax.ppermute(x, 'tx', swap)  9.13 us
    convert_element_type x3, other arithmetic, activation(): return (jax.nn.silu(gate) * up).astype(BF16)  7.93 us
  transfers between devices with their start and end apart: 3, of which 1 were waited for; matrix products, arithmetic and copies ran while one was open for 4% of the time, Pallas kernels for 25%

commit v1 on v0

--- a/solution.py
+++ b/solution.py
@@ -19,9 +19,9 @@
 EARLY = 4
 SLOTS = 4
 WCOLS = 512
-SIZES = (80, 80, 64, 32)
-STARTS = (0, 80, 160, 224)
-PIECES = (2, 4, 4, 4)
+SIZES = (80, 64, 80, 32)
+STARTS = (0, 80, 144, 224)
+PIECES = (1, 2, 4, 4)
 HBM = pl.BlockSpec(memory_space=pl.ANY)
 ATTN_ROWS = 8
 
@@ -449,7 +449,7 @@
         return pltpu.make_async_remote_copy(src.at[rel], dst.at[rel], ssem.at[rel], rsem.at[rel],
                                             device_id={'tyz': peer_of(rel)}, device_id_type=MESH)
 
-    def spread(value, src, dst, kept, ssem, rsem):
+    def spread(value, src, dst, kept, ssem, rsem, unroll=1):
         def body(step, carry):
             rel = lax.rem(step + 2, 4)
             total = value(columns(peer_of(rel), width))
@@ -465,7 +465,7 @@
 
             return carry
 
-        lax.fori_loop(0, 4, body, 0)
+        lax.fori_loop(0, 4, body, 0, unroll=unroll)
 
     outs = []
 
@@ -505,7 +505,7 @@
             finish(tx * half, *own)
             o_copy.wait_recv()
             sums[:size, :] += dot(o_got[rows, :], wo[...])
-        spread(lambda cols: sums[:size, cols] + dot(act_got[rows, last * piece:], wd[last * piece:, cols]), *blocks[idx])
+        spread(lambda cols: sums[:size, cols] + dot(act_got[rows, last * piece:], wd[last * piece:, cols]), *blocks[idx], unroll=4 if idx == 3 else 1)
         if idx > 0:
             finish(base + STARTS[idx - 1], *blocks[idx - 1])
     finish(base + STARTS[3], *blocks[3])

time: 187 us -> 186 us (level)
  no operation moved by 1% of the time
where the time goes in v1:
time: 186 us
  Pallas kernels  165 us (89%)
  waiting for transfers between devices  9.13 us (5%)
  other arithmetic  7.93 us (4%)
  starting transfers between devices  2.76 us (1%)
    pallas_call x1, Pallas kernels, tail(): pl.pallas_call(tail_kernel, out_shape=jax.ShapeDtypeStruct(residual.shape...  62.9 us
    pallas_call x1, Pallas kernels, front(): pl.pallas_call(front_kernel, out_shape=blocks + blocks + (shape((4, few,...  54.6 us
    pallas_call x1, Pallas kernels, attend(): pl.pallas_call(attend_kernel, grid_spec=pltpu.PrefetchScalarGridSpec(num_...  47.4 us
    ppermute x3, waiting for transfers between devices, pass_on(): return lax.ppermute(x, 'tx', swap)  9.13 us
    convert_element_type x3, other arithmetic, activation(): return (jax.nn.silu(gate) * up).astype(BF16)  7.93 us
  transfers between devices with their start and end apart: 3, of which 1 were waited for; matrix products, arithmetic and copies ran while one was open for 4% of the time, Pallas kernels for 25%

profile of v1, /device:TPU:0, one launch (start us, length us, event | category | flops | bytes accessed | tf_op | source)
XLA Modules:
  0.0 186.3 jit_solution(5067007146637631655)
XLA Ops:
  0.6 54.6 %front.1 = (bf16[80,8192]{1,0:T(8,128)(2,1)}, bf16[64,8192]{1,0:T(8,128)(2,1)}, bf16[80,8192]{1,0:T(8,128)(2,1)}, bf16[32,8192]{1,0:T(8,128)(2,1)}, bf16[80,8192...) custom-call(bf16[512,512]{1,0:T(8,128)(2,1)} %res_in.3, ...), custom_call_target="tpu_custom_call" | custom-call | flops 17179869184 | bytes 67108864 | tf_op jit(solution)/shard_map/front/pallas_call | solution.py:271
  55.2 0.7 collective-permute-start.2
  56.0 1.3 collective-permute-start
  57.3 0.7 collective-permute-start.1
  58.0 3.0 %fusion.9.act0_ref = bf16[80,4096]{1,0:T(8,128)(2,1)} fusion(bf16[80,8192]{1,0:T(8,128)(2,1)} %get-tuple-element.18, bf16[80,8192]{1,0:T(8,128)(2,1)} %get-tuple-element.17), kind=kLoop, calls=%fused_computation.19 | loop fusion | flops 5242880 | bytes 3276800 | tf_op jit(solution)/shard_map/convert_element_type | solution.py:524
  61.1 47.4 %attend.1 = (bf16[64,4096]{1,0:T(8,128)(2,1)}, bf16[64,1024,256]{2,1,0:T(8,128)(2,1)}, bf16[64,1024,256]{2,1,0:T(8,128)(2,1)}) custom-call(s32[64]{0:T(128)} %len_ref.1, f32[1,128]{1,0:T(1,128)} %constant.8.clone.freq_ref, bf16[4,64,1024]{2,1,0:T(8,128)(2,1)} %get-tuple-element.25.q_ref, bf16[64,256]{1,0:T(8,128)(2,1)} %get-tuple-element.26.knew_ref, ...), custom_call_target="tpu_custom_call" | custom-call | flops 8589934592 | bytes 134217728 | tf_op jit(solution)/shard_map/attend/pallas_call | solution.py:352
  108.5 0.0 collective-permute-done
  108.5 0.0 copy-start.4
  108.5 2.0 %fusion.14.act1_ref = bf16[64,4096]{1,0:T(8,128)(2,1)S(1)} fusion(bf16[64,8192]{1,0:T(8,128)(2,1)} %collective-permute-done, bf16[64,8192]{1,0:T(8,128)(2,1)} %get-tuple-element.19), kind=kLoop, calls=%fused_computation.26 | loop fusion | flops 4194304 | bytes 2621440 | tf_op jit(solution)/shard_map/convert_element_type | solution.py:524
  110.5 9.1 %collective-permute-done.1 = bf16[80,8192]{1,0:T(8,128)(2,1)} collective-permute-done((bf16[80,8192]{1,0:T(8,128)(2,1)}, bf16[80,8192]{1,0:T(8,128)(2,1)}, u32[]{:S(2)}, u32[]{:S(2)}) %collective-permute-start.1) | collective-permute-done | bytes 1310752 | tf_op jit(solution)/shard_map/ppermute | solution.py:566
  119.7 0.0 copy-done.4
  119.7 0.0 copy-start
  119.7 0.0 copy-start.1
  119.7 0.0 copy-start.2
  119.7 0.0 copy-start.3
  119.7 2.8 %fusion.8.act2_ref = bf16[80,4096]{1,0:T(8,128)(2,1)} fusion(bf16[80,8192]{1,0:T(8,128)(2,1)} %collective-permute-done.1, bf16[80,8192]{1,0:T(8,128)(2,1)S(1)} %copy-done.4), kind=kLoop, calls=%fused_computation.18 | loop fusion | flops 5242880 | bytes 3276800 | tf_op jit(solution)/shard_map/convert_element_type | solution.py:524
  122.5 0.0 collective-permute-done.2.got_ref
  122.5 0.0 copy-done
  122.5 0.0 copy-done.1
  122.5 0.0 copy-done.2
  122.5 0.0 copy-done.3
  122.6 62.9 %tail.1 = bf16[512,512]{1,0:T(8,128)(2,1)S(1)} custom-call(bf16[80,4096]{1,0:T(8,128)(2,1)S(1)} %copy-done, bf16[64,4096]{1,0:T(8,128)(2,1)S(1)} %fusion.14.act1_ref, bf16[80,4096]{1,0:T(8,128)(2,1)} %fusion.8.act2_ref, bf16[32,8192]{1,0:T(8,128)(2,1)} %collective-permute-done.2.got_ref, bf16[32,8192]{1,0:T(8,128)(2,1)S(1)} %copy-done.3, ...), custom_call_target="tpu_custom_call" | custom-call | flops 17179869184 | bytes 33554432 | tf_op jit(solution)/shard_map/tail/pallas_call | solution.py:538
  185.5 0.8 copy.17
Async XLA Ops:
  55.2 67.3 %collective-permute-start.2 = (bf16[32,8192]{1,0:T(8,128)(2,1)}, bf16[32,8192]{1,0:T(8,128)(2,1)}, u32[]{:S(2)}, u32[]{:S(2)}) collective-permute-start(bf16[32,8192]{1,0:T(8,128)(2,1)} %get-tuple-element.23), channel_id=1, source_target_pairs={{0,4},{4,0},{1,5},{5,1},{2,6},{6,2},{3,7},{7,3}} | collective-permute-start | bytes 1572872 | tf_op jit(solution)/shard_map/ppermute | solution.py:566
  56.0 52.5 %collective-permute-start = (bf16[64,8192]{1,0:T(8,128)(2,1)}, bf16[64,8192]{1,0:T(8,128)(2,1)}, u32[]{:S(2)}, u32[]{:S(2)}) collective-permute-start(bf16[64,8192]{1,0:T(8,128)(2,1)} %get-tuple-element.20), channel_id=1, source_target_pairs={{0,4},{4,0},{1,5},{5,1},{2,6},{6,2},{3,7},{7,3}} | collective-permute-start | bytes 3145736 | tf_op jit(solution)/shard_map/ppermute | solution.py:566
  57.3 62.4 %collective-permute-start.1 = (bf16[80,8192]{1,0:T(8,128)(2,1)}, bf16[80,8192]{1,0:T(8,128)(2,1)}, u32[]{:S(2)}, u32[]{:S(2)}) collective-permute-start(bf16[80,8192]{1,0:T(8,128)(2,1)} %get-tuple-element.22), channel_id=1, source_target_pairs={{0,4},{4,0},{1,5},{5,1},{2,6},{6,2},{3,7},{7,3}} | collective-permute-start | bytes 3932168 | tf_op jit(solution)/shard_map/ppermute | solution.py:566
  108.5 11.2 %copy-start.4 = (bf16[80,8192]{1,0:T(8,128)(2,1)S(1)}, bf16[80,8192]{1,0:T(8,128)(2,1)}, u32[]{:S(2)}) copy-start(bf16[80,8192]{1,0:T(8,128)(2,1)} %get-tuple-element.21) | copy-start | bytes 3932164
  119.7 2.9 %copy-start = (bf16[80,4096]{1,0:T(8,128)(2,1)S(1)}, bf16[80,4096]{1,0:T(8,128)(2,1)}, u32[]{:S(2)}) copy-start(bf16[80,4096]{1,0:T(8,128)(2,1)} %fusion.9.act0_ref) | copy-start | bytes 1966084
  119.7 2.9 %copy-start.1 = (bf16[512,512]{1,0:T(8,128)(2,1)S(1)}, bf16[512,512]{1,0:T(8,128)(2,1)}, u32[]{:S(2)}) copy-start(bf16[512,512]{1,0:T(8,128)(2,1)} %res_in.3) | copy-start | bytes 1572868
  119.7 2.9 %copy-start.2 = (bf16[64,4096]{1,0:T(8,128)(2,1)S(1)}, bf16[64,4096]{1,0:T(8,128)(2,1)}, u32[]{:S(2)}) copy-start(bf16[64,4096]{1,0:T(8,128)(2,1)} %get-tuple-element.28.att_in) | copy-start | bytes 1572868
  119.7 2.9 %copy-start.3 = (bf16[32,8192]{1,0:T(8,128)(2,1)S(1)}, bf16[32,8192]{1,0:T(8,128)(2,1)}, u32[]{:S(2)}) copy-start(bf16[32,8192]{1,0:T(8,128)(2,1)} %get-tuple-element.24.mine_ref) | copy-start | bytes 1572868
